TPU v7x, 32 devices: a whole 2x2x4 slice. The times are simulated.
32 devices in a mesh: dp: 8 (over y, x, core), tp: 4 (over z).
Axes of the slice: x: 2, y: 2, z: 4, core: 2. Of those that a mesh axis runs over, the one named last changes fastest.
Arguments:
- resid: bfloat16 [2048, 4096], P('dp'), may hold values from -6 to 6
- gain: bfloat16 [4096], replicated, may hold values from 0.25 to 1.75
- grad_q: bfloat16 [2048, 3072], P('dp', 'tp'), may hold values from -1.25 to 1.25
- w_query: bfloat16 [3072, 4096], P('tp'), may hold values from -0.375 to 0.375
- grad_in: bfloat16 [2048, 4096], P('dp'), may hold values from -2 to 2
Outputs:
- weight_grad: float32 [3072, 4096], P(('tp', 'dp'))
- gain_grad: float32 [4096], replicated
- grad_out: bfloat16 [2048, 4096], P('dp')
All inputs are finite; a program needn't handle non-finite values.
Results may differ from a plain program's by a relative error of at most 0.014.
Values may be sent and summed in bfloat16 or wider, within the bound.
A program may use at most 128 MiB of HBM per device.

v0:
```python
import functools

import jax
import jax.numpy as jnp
from jax import lax
from jax.experimental import pallas as pl
from jax.experimental.pallas import tpu as pltpu
from jax.sharding import PartitionSpec as P

MESH = pl.DeviceIdType.MESH
F32 = jnp.float32
BF16 = jnp.bfloat16
ROWS = 16
TILES = 8


def norm_rows(rows_bf, gain_f):
    rows_f = rows_bf.astype(jnp.float32)
    inv_rms = lax.rsqrt(jnp.mean(rows_f * rows_f, axis=-1, keepdims=True) + 1e-05)
    unit = rows_f * inv_rms
    return (inv_rms, unit, (unit * gain_f).astype(jnp.bfloat16))


def per_device(resid, gain, grad_q, w_query, grad_in):
    gain_f = gain.astype(jnp.float32)
    inv_rms, unit, normed = norm_rows(resid, gain_f)
    local_term = jnp.dot(grad_q, w_query, preferred_element_type=jnp.float32)
    dnormed = lax.psum(local_term.astype(jnp.bfloat16), "tp").astype(jnp.float32)
    full_grad = lax.dot_general(
        grad_q, normed, (((0,), (0,)), ((), ())), preferred_element_type=jnp.float32
    )
    weight_grad = lax.psum_scatter(full_grad, "dp", scatter_dimension=0, tiled=True)
    gain_grad = lax.psum(jnp.sum(dnormed * unit, axis=0), "dp")
    dunit = dnormed * gain_f
    inner = jnp.mean(dunit * unit, axis=-1, keepdims=True)
    grad_rows = (grad_in.astype(jnp.float32) + inv_rms * (dunit - unit * inner)).astype(
        jnp.bfloat16
    )
    return (weight_grad, gain_grad, grad_rows)


def kernel(n_dp, n_tp, resid, gain, grad_q, w_query, grad_in, wg_out, gg_out, go_out,
           wv, rv, gqv, giv, nv, part, from_mate, from_peer, gq_t, gq_p,
           fgs, fgr, keep, xs, xr, ys, yr, wgo, gacc, gslot, gz,
           w_sem, in_sem, so, ro, sp, rp, out_sem, s1, r1, s2, r2, s3, r3, wg_sem, sg, rg, sz, rz):
    dp, tp = lax.axis_index("dp"), lax.axis_index("tp")
    tokens, width = rv.shape
    heads = gqv.shape[1]
    chunks = tokens // ROWS
    steps = chunks // 2
    cols = width // TILES
    block = heads // n_dp
    h = tp // 2
    is_inner = jnp.logical_and(tp > 0, tp < n_tp - 1)
    is_outer = jnp.logical_not(is_inner)
    mate = jnp.where(is_inner, h * (n_tp - 1), 1 + h)
    peer = 2 - h
    core, xx, yy = dp % 2, (dp // 2) % 2, dp // 4
    core_mate = dp + 1 - 2 * core
    x_mate = dp + 2 - 4 * xx
    y_mate = dp + 4 - 8 * yy

    def w_copy(t):
        c = pl.ds(t * cols, cols)
        return pltpu.make_async_copy(w_query.at[:, c], wv.at[:, c], w_sem.at[t])

    gq_copy = pltpu.make_async_copy(grad_q, gqv, in_sem.at[0])
    r_copy = pltpu.make_async_copy(resid, rv, in_sem.at[1])
    gi_copy = pltpu.make_async_copy(grad_in, giv, in_sem.at[2])
    gq_copy.start()
    for t in range(TILES):
        w_copy(t).start()
    r_copy.start()
    gi_copy.start()

    barrier = pltpu.get_barrier_semaphore()
    for o in range(1, n_dp):
        pl.semaphore_signal(barrier, inc=1, device_id={"dp": (dp + o) % n_dp}, device_id_type=MESH)
    for o in range(1, n_tp):
        pl.semaphore_signal(barrier, inc=1, device_id={"tp": (tp + o) % n_tp}, device_id_type=MESH)

    def rows_of(c):
        return pl.ds(pl.multiple_of(c * ROWS, ROWS), ROWS)

    def copy_o(src, c):
        return pltpu.make_async_remote_copy(
            src_ref=src.at[rows_of(c)], dst_ref=from_mate.at[rows_of(c)],
            send_sem=so.at[c], recv_sem=ro.at[c], device_id={"tp": mate}, device_id_type=MESH)

    def copy_p(src, c):
        return pltpu.make_async_remote_copy(
            src_ref=src.at[rows_of(c)], dst_ref=from_peer.at[rows_of(c)],
            send_sem=sp.at[c], recv_sem=rp.at[c], device_id={"tp": peer}, device_id_type=MESH)

    def out_copy(src, c):
        return pltpu.make_async_copy(src.at[rows_of(c)], go_out.at[rows_of(c)], out_sem.at[c])

    def hop(src, dst, send, recv, t, to):
        return pltpu.make_async_remote_copy(
            src_ref=src.at[t], dst_ref=dst.at[t], send_sem=send.at[t], recv_sem=recv.at[t],
            device_id={"dp": to}, device_id_type=MESH)

    gq_copy.wait()
    half = tokens // 2
    for m in range(2):
        for t in range(TILES):
            if m == 0:
                w_copy(t).wait()
            c = slice(t * cols, (t + 1) * cols)
            r = slice(m * half, (m + 1) * half)
            part[r, c] = jnp.dot(gqv[r, :], wv[:, c], preferred_element_type=F32).astype(BF16)
        if m == 0:
            pl.semaphore_wait(barrier, n_dp - 1 + n_tp - 1)

        @pl.when(is_outer)
        def _():
            @pl.loop(m * steps // 2, (m + 1) * steps // 2)
            def _(k):
                copy_o(part, 2 * k + 1 - h).start()
                copy_o(part, 2 * k + h).start()

    gain_f = gain[...].astype(F32)
    r_copy.wait()

    @pl.loop(0, chunks)
    def _(c):
        r = rows_of(c)
        nv[r, :] = norm_rows(rv[r, :], gain_f)[2]

    gq_t[...] = gqv[...].T
    for v in range(2):
        for j, rel in enumerate(((0, 2, 1, 3), (0, 1, 2, 3))[v]):
            y_to = yy + (rel // 2) * (1 - 2 * yy)
            x_to = xx + (rel % 2) * (1 - 2 * xx)
            for mine in range(2):
                c_to = core if mine else 1 - core
                at = pl.multiple_of((y_to * 4 + x_to * 2 + c_to) * block, block)
                gq_p[v, mine, j * block:(j + 1) * block, :] = gq_t[pl.ds(at, block), :]
    gacc[...] = jnp.zeros_like(gacc)
    first, second = (x_mate, y_mate), (y_mate, x_mate)

    def tile_cols(t):
        return pl.ds(pl.multiple_of(t * cols, cols), cols)

    @pl.loop(0, TILES // 2)
    def _(j):
        for v in range(2):
            t = 2 * j + v
            fgs[t] = jnp.dot(gq_p[v, 0], nv[:, tile_cols(t)], preferred_element_type=F32).astype(BF16)
            hop(fgs, fgr, s1, r1, t, core_mate).start()

    def stage2(j):
        for v in range(2):
            t = 2 * j + v
            hop(fgs, fgr, s1, r1, t, core_mate).wait_recv()
            total = jnp.dot(gq_p[v, 1], nv[:, tile_cols(t)], preferred_element_type=F32)
            total = total + fgr[t].astype(F32)
            xs[t] = total[2 * block:].astype(BF16)
            hop(xs, xr, s2, r2, t, first[v]).start()
            keep[t] = total[:2 * block]

    def stage3(j):
        for v in range(2):
            t = 2 * j + v
            hop(xs, xr, s2, r2, t, first[v]).wait_recv()
            ys[t] = (keep[t, block:] + xr[t, block:].astype(F32)).astype(BF16)
            hop(ys, yr, s3, r3, t, second[v]).start()
            keep[t, :block] = keep[t, :block] + xr[t, :block].astype(F32)

    def wg_copy(t):
        return pltpu.make_async_copy(wgo.at[t], wg_out.at[:, tile_cols(t)], wg_sem.at[t])

    def stage4(j):
        for v in range(2):
            t = 2 * j + v
            hop(ys, yr, s3, r3, t, second[v]).wait_recv()
            wgo[t] = keep[t, :block] + yr[t].astype(F32)
            wg_copy(t).start()

    gi_copy.wait()

    def forward(k):
        b = 2 * k + 1 - h
        copy_p(from_peer, b).wait_recv()
        copy_o(from_peer, b).start()
        out_copy(from_peer, b).start()

    def collect(k):
        for c in (2 * k + h, 2 * k + 1 - h):
            copy_o(from_mate, c).wait_recv()
            out_copy(from_mate, c).start()

    def pass_on(k):
        b = rows_of(2 * k + 1 - h)
        copy_o(part, 2 * k + 1 - h).wait_recv()
        part[b, :] = (part[b, :].astype(F32) + from_mate[b, :].astype(F32)).astype(BF16)
        copy_p(part, 2 * k + 1 - h).start()

    def finish(k):
        a = 2 * k + h
        copy_o(part, a).wait_recv()
        copy_p(part, a).wait_recv()
        r = rows_of(a)
        inv_rms, unit, _ = norm_rows(rv[r, :], gain_f)
        dnormed = part[r, :].astype(F32) + from_mate[r, :].astype(F32)
        dnormed = dnormed + from_peer[r, :].astype(F32)
        gacc[...] += jnp.sum(dnormed * unit, axis=0, keepdims=True)
        dunit = dnormed * gain_f
        mean = jnp.mean(dunit * unit, axis=-1, keepdims=True)
        part[r, :] = (
            giv[r, :].astype(F32) + inv_rms * (dunit - unit * mean)
        ).astype(BF16)
        copy_p(part, a).start()
        copy_o(part, a).start()
        out_copy(part, a).start()

    @pl.loop(0, steps + 1)
    def _(k):
        @pl.when(jnp.logical_and(is_inner, k < steps))
        def _():
            pass_on(k)

        @pl.when(jnp.logical_and(is_inner, k > 0))
        def _():
            finish(k - 1)

        @pl.when(jnp.logical_and(is_inner, k > 1))
        def _():
            forward(k - 2)

        @pl.when(jnp.logical_and(is_outer, k > 2))
        def _():
            collect(k - 3)

        @pl.when(k < 2)
        def _():
            stage2(2 * k)
            stage2(2 * k + 1)

        @pl.when(jnp.logical_and(k >= 2, k < 2 + TILES // 2))
        def _():
            stage3(k - 2)

        @pl.when(jnp.logical_and(k >= 4, k < 4 + TILES // 2))
        def _():
            stage4(k - 4)

    def g_copy(o):
        return pltpu.make_async_remote_copy(
            src_ref=gslot.at[0], dst_ref=gslot.at[o], send_sem=sg.at[o], recv_sem=rg.at[o],
            device_id={"dp": (dp + o) % n_dp}, device_id_type=MESH)

    def z_copy(i, to):
        return pltpu.make_async_remote_copy(
            src_ref=gz.at[h], dst_ref=gz.at[h], send_sem=sz.at[i], recv_sem=rz.at[h],
            device_id={"tp": to}, device_id_type=MESH)

    def z_wait(which):
        pltpu.make_async_remote_copy(
            src_ref=gz.at[which], dst_ref=gz.at[which], send_sem=sz.at[0], recv_sem=rz.at[which],
            device_id={"tp": mate}, device_id_type=MESH).wait_recv()

    @pl.when(is_inner)
    def _():
        gslot[0] = gacc[...]
        for o in range(1, n_dp):
            g_copy(o).start()
        forward(steps - 1)
        for o in range(1, n_dp):
            g_copy(o).wait_recv()
        total = gslot[dp % n_dp]
        for d in range(1, n_dp):
            total = total + gslot[(dp + n_dp - d) % n_dp]
        gz[h] = total
        targets = (mate, peer, (1 - h) * (n_tp - 1))
        for i, to in enumerate(targets):
            z_copy(i, to).start()
        z_wait(1 - h)
        gg_out[...] = gz[0] + gz[1]
        for i, to in enumerate(targets):
            z_copy(i, to).wait_send()
        for o in range(1, n_dp):
            g_copy(o).wait_send()

        @pl.loop(0, chunks)
        def _(c):
            copy_p(part, c).wait_send()

    @pl.when(is_outer)
    def _():
        for k in range(steps - 2, steps):
            collect(k)
        z_wait(0)
        z_wait(1)
        gg_out[...] = gz[0] + gz[1]

    @pl.loop(0, chunks)
    def _(c):
        copy_o(part, c).wait_send()
        out_copy(part, c).wait()

    for t in range(TILES):
        hop(fgs, fgr, s1, r1, t, core_mate).wait_send()
        hop(xs, xr, s2, r2, t, first[t % 2]).wait_send()
        hop(ys, yr, s3, r3, t, second[t % 2]).wait_send()
        wg_copy(t).wait()


def fused(n_dp, n_tp, resid, gain, grad_q, w_query, grad_in):
    tokens, width = resid.shape
    heads = grad_q.shape[1]
    chunks = tokens // ROWS
    block, cols = heads // n_dp, width // TILES
    any_space = pl.BlockSpec(memory_space=pl.ANY)
    vmem = pl.BlockSpec(memory_space=pltpu.VMEM)
    dma = lambda n: pltpu.SemaphoreType.DMA((n,))
    weight_grad, gain_grad, grad_rows = pl.pallas_call(
        functools.partial(kernel, n_dp, n_tp),
        out_shape=(
            jax.ShapeDtypeStruct((block, width), F32),
            jax.ShapeDtypeStruct((1, width), F32),
            jax.ShapeDtypeStruct((tokens, width), BF16),
        ),
        in_specs=[any_space, vmem, any_space, any_space, any_space],
        out_specs=(any_space, vmem, any_space),
        scratch_shapes=[
            pltpu.VMEM((heads, width), BF16),
            pltpu.VMEM((tokens, width), BF16),
            pltpu.VMEM((tokens, heads), BF16),
            pltpu.VMEM((tokens, width), BF16),
            pltpu.VMEM((tokens, width), BF16),
            pltpu.VMEM((tokens, width), BF16),
            pltpu.VMEM((tokens, width), BF16),
            pltpu.VMEM((tokens, width), BF16),
            pltpu.VMEM((heads, tokens), BF16),
            pltpu.VMEM((2, 2, 4 * block, tokens), BF16),
            pltpu.VMEM((TILES, 4 * block, cols), BF16),
            pltpu.VMEM((TILES, 4 * block, cols), BF16),
            pltpu.VMEM((TILES, 2 * block, cols), F32),
            pltpu.VMEM((TILES, 2 * block, cols), BF16),
            pltpu.VMEM((TILES, 2 * block, cols), BF16),
            pltpu.VMEM((TILES, block, cols), BF16),
            pltpu.VMEM((TILES, block, cols), BF16),
            pltpu.VMEM((TILES, block, cols), F32),
            pltpu.VMEM((1, width), F32),
            pltpu.VMEM((n_dp, 1, width), F32),
            pltpu.VMEM((2, 1, width), F32),
            dma(TILES), dma(3), dma(chunks), dma(chunks), dma(chunks), dma(chunks), dma(chunks),
            dma(TILES), dma(TILES), dma(TILES), dma(TILES), dma(TILES), dma(TILES), dma(TILES),
            dma(n_dp), dma(n_dp), dma(3), dma(2),
        ],
        compiler_params=pltpu.CompilerParams(
            collective_id=0, has_side_effects=True, vmem_limit_bytes=60 * 1024 * 1024
        ),
    )(resid, gain.reshape(1, width), grad_q, w_query, grad_in)
    return weight_grad, gain_grad.reshape(width), grad_rows


def solution(mesh):
    n_dp, n_tp = mesh.shape["dp"], mesh.shape["tp"]
    if (n_dp, n_tp) == (2 * 2 * 2, 4):
        body = functools.partial(fused, n_dp, n_tp)
    else:
        body = per_device
    return jax.shard_map(
        body,
        mesh=mesh,
        in_specs=(P("dp", None), P(), P("dp", "tp"), P("tp", None), P("dp", None)),
        out_specs=(P(("tp", "dp"), None), P(), P("dp", None)),
        check_vma=False,
    )
```

profile of v0, /device:TPU:0, one launch (start us, length us, event | category | flops | bytes accessed | tf_op | source)
XLA Modules:
  0.0 76.9 jit_solution(15025582604231926536)
XLA Ops:
  0.6 1.3 %reshape.12.gain = bf16[1,4096]{1,0:T(2,128)(2,1)} reshape(bf16[4096]{0:T(1024)(128)(2,1)} %param.6) | data formatting | bytes 16384 | tf_op jit(solution)/shard_map/reshape | solution.py:355
  1.9 70.2 %shard_map.76 = (f32[96,4096]{1,0:T(8,128)}, f32[1,4096]{1,0:T(1,128)}, bf16[256,4096]{1,0:T(8,128)(2,1)}) custom-call(bf16[256,4096]{1,0:T(8,128)(2,1)} %resid.1, bf16[1,4096]{1,0:T(2,128)(2,1)} %reshape.12.gain, bf16[256,768]{1,0:T(8,128)(2,1)} %grad_q.1, bf16[768,4096]{1,0:T(8,128)(2,1)} %w_query.1, bf16[256,4096]{1,0:T(8,128)(2,1)} %grad_in.1), custom_call_target="tpu_custom_call" | custom-call | tf_op jit(solution)/shard_map/pallas_call | solution.py:317
  72.1 0.0 copy-start.1
  72.1 0.0 copy-start
  72.1 2.8 %copy.11 = f32[96,4096]{1,0:T(8,128)} copy(f32[96,4096]{1,0:T(8,128)} %get-tuple-element.12) | data formatting | bytes 3145728
  74.9 0.0 copy-done.1
  74.9 0.6 copy.12
  75.6 0.0 copy-done
  75.6 1.3 %copy.13 = bf16[256,4096]{1,0:T(8,128)(2,1)} copy(bf16[256,4096]{1,0:T(8,128)(2,1)S(1)} %copy-done) | data formatting | bytes 4194304
Async XLA Ops:
  72.1 2.8 %copy-start.1 = (f32[1,4096]{1,0:T(1,128)S(1)}, f32[1,4096]{1,0:T(1,128)}, u32[]{:S(2)}) copy-start(f32[1,4096]{1,0:T(1,128)} %get-tuple-element.7) | copy-start | bytes 49156
  72.1 3.4 %copy-start = (bf16[256,4096]{1,0:T(8,128)(2,1)S(1)}, bf16[256,4096]{1,0:T(8,128)(2,1)}, u32[]{:S(2)}) copy-start(bf16[256,4096]{1,0:T(8,128)(2,1)} %get-tuple-element.14) | copy-start | bytes 6291460
where the time goes:
time: 77.2 us; the launch traced here: 76.9 us
  Pallas kernels  70.2 us (91%)
  local copies, waits for them, and re-layouts  6.05 us (8%)
    pallas_call x1, Pallas kernels, fused(): pl.pallas_call(functools.partial(kernel, n_dp, n_tp), out_shape=(jax.Shap...  70.2 us
    unnamed x7, local copies, waits for them, and re-layouts  4.74 us

commit v1 on v0

v1 whole, which is shorter than its diff:
```python
import functools

import jax
import jax.numpy as jnp
from jax import lax
from jax.experimental import pallas as pl
from jax.experimental.pallas import tpu as pltpu
from jax.sharding import PartitionSpec as P

MESH = pl.DeviceIdType.MESH
F32 = jnp.float32
BF16 = jnp.bfloat16
ROWS = 16
TILES = 8
QUARTERS = 4
FIRST = 2
LAG = 4


def norm_rows(rows_bf, gain_f):
    rows_f = rows_bf.astype(jnp.float32)
    inv_rms = lax.rsqrt(jnp.mean(rows_f * rows_f, axis=-1, keepdims=True) + 1e-05)
    unit = rows_f * inv_rms
    return (inv_rms, unit, (unit * gain_f).astype(jnp.bfloat16))


def per_device(resid, gain, grad_q, w_query, grad_in):
    gain_f = gain.astype(jnp.float32)
    inv_rms, unit, normed = norm_rows(resid, gain_f)
    local_term = jnp.dot(grad_q, w_query, preferred_element_type=jnp.float32)
    dnormed = lax.psum(local_term.astype(jnp.bfloat16), "tp").astype(jnp.float32)
    full_grad = lax.dot_general(
        grad_q, normed, (((0,), (0,)), ((), ())), preferred_element_type=jnp.float32
    )
    weight_grad = lax.psum_scatter(full_grad, "dp", scatter_dimension=0, tiled=True)
    gain_grad = lax.psum(jnp.sum(dnormed * unit, axis=0), "dp")
    dunit = dnormed * gain_f
    inner = jnp.mean(dunit * unit, axis=-1, keepdims=True)
    grad_rows = (grad_in.astype(jnp.float32) + inv_rms * (dunit - unit * inner)).astype(
        jnp.bfloat16
    )
    return (weight_grad, gain_grad, grad_rows)


def kernel(n_dp, n_tp, resid, gain, grad_q, w_query, grad_in, wg_out, gg_out, go_out,
           wv, rv, gqv, giv, nv, part, from_mate, from_peer, ds, gov, gain_f, inv, gq_t, gq_p,
           fgs, fgr, keep, xs, xr, ys, yr, wgo, gacc, gslot, gz,
           w_sem, in_sem, r_sem, gi_sem, so, sp, rm, rp, out_sem,
           s1, r1, s2, r2, s3, r3, wg_sem, sg, rg, sz, rz):
    dp, tp = lax.axis_index("dp"), lax.axis_index("tp")
    _, tokens, span = rv.shape
    heads = gqv.shape[1]
    width = QUARTERS * span
    chunks = tokens // ROWS
    cols = width // TILES
    block = heads // n_dp
    h = tp // 2
    is_inner = jnp.logical_and(tp > 0, tp < n_tp - 1)
    is_outer = jnp.logical_not(is_inner)
    mate = jnp.where(is_inner, h * (n_tp - 1), 1 + h)
    peer = 2 - h
    core, xx, yy = dp % 2, (dp // 2) % 2, dp // 4
    core_mate = dp + 1 - 2 * core
    x_mate = dp + 2 - 4 * xx
    y_mate = dp + 4 - 8 * yy
    own, other = 2 * h, 2 - 2 * h
    turns = ((other, 0), (own, 0), (other, 1), (own, 1))

    def span_of(a):
        return pl.ds(pl.multiple_of(a * span, span), span)

    def w_copy(s):
        a = turns[s][0] + turns[s][1]
        return pltpu.make_async_copy(w_query.at[:, span_of(a)], wv.at[a], w_sem.at[s])

    def r_copy(a):
        return pltpu.make_async_copy(
            resid.at[:, a * span:(a + 1) * span], rv.at[a], r_sem.at[a])

    def gi_copy(a):
        return pltpu.make_async_copy(
            grad_in.at[:, a * span:(a + 1) * span], giv.at[a], gi_sem.at[a])

    gq_copy = pltpu.make_async_copy(grad_q, gqv, in_sem.at[0])
    gq_copy.start()
    for s in range(QUARTERS):
        w_copy(s).start()

    barrier = pltpu.get_barrier_semaphore()
    for to in (core_mate, x_mate, y_mate):
        pl.semaphore_signal(barrier, inc=1, device_id={"dp": to}, device_id_type=MESH)
    pl.semaphore_signal(barrier, inc=1, device_id={"tp": mate}, device_id_type=MESH)

    @pl.when(is_inner)
    def _():
        pl.semaphore_signal(barrier, inc=1, device_id={"tp": peer}, device_id_type=MESH)

    def rows_of(c):
        return pl.ds(pl.multiple_of(c * ROWS, ROWS), ROWS)

    def to_mate(src, dst, a, c):
        return pltpu.make_async_remote_copy(
            src_ref=src.at[a, rows_of(c)], dst_ref=dst.at[a, rows_of(c)],
            send_sem=so.at[0], recv_sem=rm.at[QUARTERS * c + a],
            device_id={"tp": mate}, device_id_type=MESH)

    def to_peer(src, dst, a, c):
        return pltpu.make_async_remote_copy(
            src_ref=src.at[a, rows_of(c)], dst_ref=dst.at[a, rows_of(c)],
            send_sem=sp.at[0], recv_sem=rp.at[QUARTERS * c + a],
            device_id={"tp": peer}, device_id_type=MESH)

    def hop(src, dst, send, recv, t, to):
        return pltpu.make_async_remote_copy(
            src_ref=src.at[t], dst_ref=dst.at[t], send_sem=send.at[t], recv_sem=recv.at[t],
            device_id={"dp": to}, device_id_type=MESH)

    gq_copy.wait()
    head = FIRST * ROWS
    for s, (base, q) in enumerate(turns):
        a = base + q
        w_copy(s).wait()
        part[a, :head, :] = jnp.dot(
            gqv[:head, :], wv[a], preferred_element_type=F32).astype(BF16)
        if s == 0:
            @pl.when(is_inner)
            def _():
                pl.semaphore_wait(barrier, 5)

            @pl.when(is_outer)
            def _():
                pl.semaphore_wait(barrier, 4)

        @pl.when(is_outer)
        def _():
            for c in range(FIRST):
                to_mate(part, from_mate, a, c).start()

    for a in range(QUARTERS):
        r_copy(a).start()
    for a in range(QUARTERS):
        gi_copy(a).start()

    for base, q in turns:
        a = base + q
        part[a, head:, :] = jnp.dot(
            gqv[head:, :], wv[a], preferred_element_type=F32).astype(BF16)

    @pl.when(is_outer)
    def _():
        @pl.loop(FIRST, chunks)
        def _(c):
            for base in (other, own):
                for q in range(2):
                    to_mate(part, from_mate, base + q, c).start()

    for a in range(QUARTERS):
        gain_f[a] = gain[:, a * span:(a + 1) * span].astype(F32)
        r_copy(a).wait()
        gi_copy(a).wait()
    gacc[...] = jnp.zeros_like(gacc)

    def norm(c):
        r = rows_of(c)
        total = jnp.zeros((ROWS, span), F32)
        for a in range(QUARTERS):
            x = rv[a, r, :].astype(F32)
            total = total + x * x
        scale = lax.rsqrt(jnp.sum(total, axis=-1, keepdims=True) * (1.0 / width) + 1e-05)
        inv[r, :] = scale
        for a in range(QUARTERS):
            nv[a, r, :] = (rv[a, r, :].astype(F32) * scale * gain_f[a]).astype(BF16)

    def regroup():
        gq_t[...] = gqv[...].T
        for v in range(2):
            for j, rel in enumerate(((0, 2, 1, 3), (0, 1, 2, 3))[v]):
                y_to = yy + (rel // 2) * (1 - 2 * yy)
                x_to = xx + (rel % 2) * (1 - 2 * xx)
                for mine in range(2):
                    c_to = core if mine else 1 - core
                    at = pl.multiple_of((y_to * 4 + x_to * 2 + c_to) * block, block)
                    gq_p[v, mine, j * block:(j + 1) * block, :] = gq_t[pl.ds(at, block), :]

    first, second = (x_mate, y_mate), (y_mate, x_mate)

    def product(mine, j, v):
        return jnp.dot(gq_p[v, mine], nv[j, :, v * cols:(v + 1) * cols], preferred_element_type=F32)

    def stage1(j):
        for v in range(2):
            t = 2 * j + v
            fgs[t] = product(0, j, v).astype(BF16)
            hop(fgs, fgr, s1, r1, t, core_mate).start()

    def stage2(j):
        for v in range(2):
            t = 2 * j + v
            hop(fgs, fgr, s1, r1, t, core_mate).wait_recv()
            total = product(1, j, v) + fgr[t].astype(F32)
            xs[t] = total[2 * block:].astype(BF16)
            hop(xs, xr, s2, r2, t, first[v]).start()
            keep[t] = total[:2 * block]

    def stage3(j):
        for v in range(2):
            t = 2 * j + v
            hop(xs, xr, s2, r2, t, first[v]).wait_recv()
            ys[t] = (keep[t, block:] + xr[t, block:].astype(F32)).astype(BF16)
            hop(ys, yr, s3, r3, t, second[v]).start()
            keep[t, :block] = keep[t, :block] + xr[t, :block].astype(F32)

    def wg_copy(t):
        return pltpu.make_async_copy(
            wgo.at[t], wg_out.at[:, pl.ds(pl.multiple_of(t * cols, cols), cols)], wg_sem.at[t])

    def stage4(j):
        for v in range(2):
            t = 2 * j + v
            hop(ys, yr, s3, r3, t, second[v]).wait_recv()
            wgo[t] = keep[t, :block] + yr[t].astype(F32)
            wg_copy(t).start()

    def pass_on(c):
        for q in range(2):
            a = other + q
            to_mate(part, from_mate, a, c).wait_recv()
            r = rows_of(c)
            part[a, r, :] = (
                part[a, r, :].astype(F32) + from_mate[a, r, :].astype(F32)).astype(BF16)
            to_peer(part, from_peer, a, c).start()

    def root(c):
        for q in range(2):
            a = own + q
            to_mate(part, from_mate, a, c).wait_recv()
            to_peer(part, from_peer, a, c).wait_recv()
            r = rows_of(c)
            dnormed = part[a, r, :].astype(F32) + from_mate[a, r, :].astype(F32)
            dnormed = dnormed + from_peer[a, r, :].astype(F32)
            ds[a, r, :] = dnormed.astype(BF16)
            to_mate(ds, ds, a, c).start()
            to_peer(ds, ds, a, c).start()
            term = dnormed * (rv[a, r, :].astype(F32) * inv[r, :])
            gacc[q] += term[:8] + term[8:]

    def forward(c):
        for q in range(2):
            a = other + q
            to_peer(ds, ds, a, c).wait_recv()
            to_mate(ds, ds, a, c).start()

    def collect(c):
        for a in range(QUARTERS):
            to_mate(part, ds, a, c).wait_recv()

    def out_copy(a, c):
        return pltpu.make_async_copy(
            gov.at[a, rows_of(c)], go_out.at[rows_of(c), a * span:(a + 1) * span],
            out_sem.at[QUARTERS * c + a])

    def finish(c):
        r = rows_of(c)
        scale = inv[r, :]
        total = jnp.zeros((ROWS, span), F32)
        for a in range(QUARTERS):
            total = total + ds[a, r, :].astype(F32) * gain_f[a] * (rv[a, r, :].astype(F32) * scale)
        mean = jnp.sum(total, axis=-1, keepdims=True) * (1.0 / width)
        for a in range(QUARTERS):
            dunit = ds[a, r, :].astype(F32) * gain_f[a]
            unit = rv[a, r, :].astype(F32) * scale
            gov[a, r, :] = (
                giv[a, r, :].astype(F32) + scale * (dunit - unit * mean)).astype(BF16)
            out_copy(a, c).start()

    def g_copy(o):
        return pltpu.make_async_remote_copy(
            src_ref=gslot.at[0], dst_ref=gslot.at[o], send_sem=sg.at[o], recv_sem=rg.at[o],
            device_id={"dp": (dp + o) % n_dp}, device_id_type=MESH)

    targets = (mate, peer, (1 - h) * (n_tp - 1))

    def z_copy(i):
        return pltpu.make_async_remote_copy(
            src_ref=gz.at[h], dst_ref=gz.at[h], send_sem=sz.at[i], recv_sem=rz.at[h],
            device_id={"tp": targets[i]}, device_id_type=MESH)

    def z_wait(which):
        pltpu.make_async_remote_copy(
            src_ref=gz.at[which], dst_ref=gz.at[which], send_sem=sz.at[0], recv_sem=rz.at[which],
            device_id={"tp": mate}, device_id_type=MESH).wait_recv()

    def at(i, lo, hi):
        return jnp.logical_and(i >= lo, i < hi)

    @pl.loop(0, chunks + LAG)
    def _(i):
        @pl.when(jnp.logical_and(is_inner, i < chunks))
        def _():
            pass_on(i)

        @pl.when(jnp.logical_and(is_inner, at(i, 1, chunks + 1)))
        def _():
            root(i - 1)

        @pl.when(jnp.logical_and(is_inner, i == chunks))
        def _():
            for q in range(2):
                gslot[0, q:q + 1, :] = jnp.sum(gacc[q], axis=0, keepdims=True)
            for o in range(1, n_dp):
                g_copy(o).start()

        @pl.when(jnp.logical_and(is_inner, at(i, 2, chunks + 2)))
        def _():
            forward(i - 2)

        @pl.when(jnp.logical_and(is_inner, at(i, 3, chunks + 3)))
        def _():
            finish(i - 3)

        @pl.when(jnp.logical_and(is_outer, i >= LAG))
        def _():
            collect(i - LAG)
            finish(i - LAG)

        @pl.when(i == 0)
        def _():
            pl.loop(0, 9)(norm)

        @pl.when(i == 1)
        def _():
            pl.loop(9, 13)(norm)

        @pl.when(i == 2)
        def _():
            pl.loop(13, chunks)(norm)
            regroup()

        @pl.when(at(i, 3, 5))
        def _():
            stage1(2 * (i - 3))
            stage1(2 * (i - 3) + 1)

        @pl.when(at(i, 5, 9))
        def _():
            stage2(i - 5)

        @pl.when(at(i, 9, 13))
        def _():
            stage3(i - 9)

        @pl.when(at(i, 13, 17))
        def _():
            stage4(i - 13)

    @pl.when(is_inner)
    def _():
        for o in range(1, n_dp):
            g_copy(o).wait_recv()
        total = gslot[dp % n_dp]
        for d in range(1, n_dp):
            total = total + gslot[(dp + n_dp - d) % n_dp]
        gz[h] = total
        for i in range(3):
            z_copy(i).start()
        z_wait(1 - h)
        for i in range(3):
            z_copy(i).wait_send()
        for o in range(1, n_dp):
            g_copy(o).wait_send()
        pltpu.make_async_remote_copy(
            src_ref=part, dst_ref=ds, send_sem=sp.at[0], recv_sem=rp.at[0],
            device_id={"tp": peer}, device_id_type=MESH).wait_send()

    @pl.when(is_outer)
    def _():
        z_wait(0)
        z_wait(1)

    for a in range(QUARTERS):
        gg_out[:, a * span:(a + 1) * span] = gz[a // 2, a % 2:a % 2 + 1, :]
    pltpu.make_async_remote_copy(
        src_ref=part, dst_ref=ds, send_sem=so.at[0], recv_sem=rm.at[0],
        device_id={"tp": mate}, device_id_type=MESH).wait_send()

    @pl.loop(0, chunks)
    def _(c):
        for a in range(QUARTERS):
            out_copy(a, c).wait()

    for t in range(TILES):
        hop(fgs, fgr, s1, r1, t, core_mate).wait_send()
        hop(xs, xr, s2, r2, t, first[t % 2]).wait_send()
        hop(ys, yr, s3, r3, t, second[t % 2]).wait_send()
        wg_copy(t).wait()


def fused(n_dp, n_tp, resid, gain, grad_q, w_query, grad_in):
    tokens, width = resid.shape
    heads = grad_q.shape[1]
    chunks = tokens // ROWS
    block, cols, span = heads // n_dp, width // TILES, width // QUARTERS
    any_space = pl.BlockSpec(memory_space=pl.ANY)
    vmem = pl.BlockSpec(memory_space=pltpu.VMEM)
    dma = lambda n: pltpu.SemaphoreType.DMA((n,))
    wide = lambda: pltpu.VMEM((QUARTERS, tokens, span), BF16)
    weight_grad, gain_grad, grad_rows = pl.pallas_call(
        functools.partial(kernel, n_dp, n_tp),
        out_shape=(
            jax.ShapeDtypeStruct((block, width), F32),
            jax.ShapeDtypeStruct((1, width), F32),
            jax.ShapeDtypeStruct((tokens, width), BF16),
        ),
        in_specs=[any_space, vmem, any_space, any_space, any_space],
        out_specs=(any_space, vmem, any_space),
        scratch_shapes=[
            pltpu.VMEM((QUARTERS, heads, span), BF16),
            wide(),
            pltpu.VMEM((tokens, heads), BF16),
            wide(), wide(), wide(), wide(), wide(), wide(), wide(),
            pltpu.VMEM((QUARTERS, 1, span), F32),
            pltpu.VMEM((tokens, 1), F32),
            pltpu.VMEM((heads, tokens), BF16),
            pltpu.VMEM((2, 2, 4 * block, tokens), BF16),
            pltpu.VMEM((TILES, 4 * block, cols), BF16),
            pltpu.VMEM((TILES, 4 * block, cols), BF16),
            pltpu.VMEM((TILES, 2 * block, cols), F32),
            pltpu.VMEM((TILES, 2 * block, cols), BF16),
            pltpu.VMEM((TILES, 2 * block, cols), BF16),
            pltpu.VMEM((TILES, block, cols), BF16),
            pltpu.VMEM((TILES, block, cols), BF16),
            pltpu.VMEM((TILES, block, cols), F32),
            pltpu.VMEM((2, 8, span), F32),
            pltpu.VMEM((n_dp, 2, span), F32),
            pltpu.VMEM((2, 2, span), F32),
            dma(QUARTERS), dma(1), dma(QUARTERS), dma(QUARTERS), dma(1), dma(1),
            dma(QUARTERS * chunks), dma(QUARTERS * chunks), dma(QUARTERS * chunks),
            dma(TILES), dma(TILES), dma(TILES), dma(TILES), dma(TILES), dma(TILES), dma(TILES),
            dma(n_dp), dma(n_dp), dma(3), dma(2),
        ],
        compiler_params=pltpu.CompilerParams(
            collective_id=0, has_side_effects=True, vmem_limit_bytes=60 * 1024 * 1024
        ),
    )(resid, gain.reshape(1, width), grad_q, w_query, grad_in)
    return weight_grad, gain_grad.reshape(width), grad_rows


def solution(mesh):
    n_dp, n_tp = mesh.shape["dp"], mesh.shape["tp"]
    if (n_dp, n_tp) == (2 * 2 * 2, 4):
        body = functools.partial(fused, n_dp, n_tp)
    else:
        body = per_device
    return jax.shard_map(
        body,
        mesh=mesh,
        in_specs=(P("dp", None), P(), P("dp", "tp"), P("tp", None), P("dp", None)),
        out_specs=(P(("tp", "dp"), None), P(), P("dp", None)),
        check_vma=False,
    )
```

time: 77.2 us -> 74.2 us (0.961)
  Pallas kernels: 70.2 us -> 67.2 us
    pallas_call x1, Pallas kernels: 70.2 us -> 67.2 us  [fused(): pl.pallas_call(functools.partial(kernel, n_dp, n_tp), out_shape=(jax.Shap...]
where the time goes in v1:
time: 74.2 us; the launch traced here: 73.9 us
  Pallas kernels  67.2 us (91%)
  local copies, waits for them, and re-layouts  6.05 us (8%)
    pallas_call x1, Pallas kernels, fused(): pl.pallas_call(functools.partial(kernel, n_dp, n_tp), out_shape=(jax.Shap...  67.2 us
    unnamed x7, local copies, waits for them, and re-layouts  4.74 us

profile of v1, /device:TPU:0, one launch (start us, length us, event | category | flops | bytes accessed | tf_op | source)
XLA Modules:
  0.0 73.9 jit_solution(487739558923967664)
XLA Ops:
  0.6 1.3 %reshape.12.gain = bf16[1,4096]{1,0:T(2,128)(2,1)} reshape(bf16[4096]{0:T(1024)(128)(2,1)} %param.6) | data formatting | bytes 16384 | tf_op jit(solution)/shard_map/reshape | solution.py:444
  1.9 67.2 %shard_map.76 = (f32[96,4096]{1,0:T(8,128)}, f32[1,4096]{1,0:T(1,128)}, bf16[256,4096]{1,0:T(8,128)(2,1)}) custom-call(bf16[256,4096]{1,0:T(8,128)(2,1)} %resid.1, bf16[1,4096]{1,0:T(2,128)(2,1)} %reshape.12.gain, bf16[256,768]{1,0:T(8,128)(2,1)} %grad_q.1, bf16[768,4096]{1,0:T(8,128)(2,1)} %w_query.1, bf16[256,4096]{1,0:T(8,128)(2,1)} %grad_in.1), custom_call_target="tpu_custom_call" | custom-call | tf_op jit(solution)/shard_map/pallas_call | solution.py:407
  69.1 0.0 copy-start.1
  69.1 0.0 copy-start
  69.1 2.8 %copy.11 = f32[96,4096]{1,0:T(8,128)} copy(f32[96,4096]{1,0:T(8,128)} %get-tuple-element.12) | data formatting | bytes 3145728
  71.9 0.0 copy-done.1
  71.9 0.6 copy.12
  72.5 0.0 copy-done
  72.5 1.3 %copy.13 = bf16[256,4096]{1,0:T(8,128)(2,1)} copy(bf16[256,4096]{1,0:T(8,128)(2,1)S(1)} %copy-done) | data formatting | bytes 4194304
Async XLA Ops:
  69.1 2.8 %copy-start.1 = (f32[1,4096]{1,0:T(1,128)S(1)}, f32[1,4096]{1,0:T(1,128)}, u32[]{:S(2)}) copy-start(f32[1,4096]{1,0:T(1,128)} %get-tuple-element.7) | copy-start | bytes 49156
  69.1 3.4 %copy-start = (bf16[256,4096]{1,0:T(8,128)(2,1)S(1)}, bf16[256,4096]{1,0:T(8,128)(2,1)}, u32[]{:S(2)}) copy-start(bf16[256,4096]{1,0:T(8,128)(2,1)} %get-tuple-element.14) | copy-start | bytes 6291460

commit v2 on v1

--- a/solution.py
+++ b/solution.py
@@ -13,8 +13,10 @@
 ROWS = 16
 TILES = 8
 QUARTERS = 4
-FIRST = 2
-LAG = 4
+LEAD = 2
+FIRST = LEAD + 1
+VMEM_MIB = 52
+LAG = 6
 
 
 def norm_rows(rows_bf, gain_f):
@@ -42,11 +44,11 @@
     return (weight_grad, gain_grad, grad_rows)
 
 
-def kernel(n_dp, n_tp, resid, gain, grad_q, w_query, grad_in, wg_out, gg_out, go_out,
-           wv, rv, gqv, giv, nv, part, from_mate, from_peer, ds, gov, gain_f, inv, gq_t, gq_p,
-           fgs, fgr, keep, xs, xr, ys, yr, wgo, gacc, gslot, gz,
-           w_sem, in_sem, r_sem, gi_sem, so, sp, rm, rp, out_sem,
-           s1, r1, s2, r2, s3, r3, wg_sem, sg, rg, sz, rz):
+def kernel(n_dp, n_tp, resid, gain, grad_q, w_query, grad_in, wgo, ggv, gov,
+           wv, rv, gqv, giv, nv, part, from_mate, from_peer, ds, gain_v, gain_f, inv, gq_t, gq_p,
+           fgs, fgr, keep, xs, xr, ys, yr, gacc, gslot, gz,
+           w_sem, in_sem, r_sem, gi_sem, so, sp, rm, rp,
+           s1, r1, s2, r2, s3, r3, sg, rg, sz, rz):
     dp, tp = lax.axis_index("dp"), lax.axis_index("tp")
     _, tokens, span = rv.shape
     heads = gqv.shape[1]
@@ -64,7 +66,7 @@
     x_mate = dp + 2 - 4 * xx
     y_mate = dp + 4 - 8 * yy
     own, other = 2 * h, 2 - 2 * h
-    turns = ((other, 0), (own, 0), (other, 1), (own, 1))
+    turns = ((other, 0), (other, 1), (own, 0), (own, 1))
 
     def span_of(a):
         return pl.ds(pl.multiple_of(a * span, span), span)
@@ -82,7 +84,9 @@
             grad_in.at[:, a * span:(a + 1) * span], giv.at[a], gi_sem.at[a])
 
     gq_copy = pltpu.make_async_copy(grad_q, gqv, in_sem.at[0])
+    gain_copy = pltpu.make_async_copy(gain, gain_v, in_sem.at[1])
     gq_copy.start()
+    gain_copy.start()
     for s in range(QUARTERS):
         w_copy(s).start()
 
@@ -98,16 +102,16 @@
     def rows_of(c):
         return pl.ds(pl.multiple_of(c * ROWS, ROWS), ROWS)
 
-    def to_mate(src, dst, a, c):
+    def to_mate(src, dst, base, c):
         return pltpu.make_async_remote_copy(
-            src_ref=src.at[a, rows_of(c)], dst_ref=dst.at[a, rows_of(c)],
-            send_sem=so.at[0], recv_sem=rm.at[QUARTERS * c + a],
+            src_ref=src.at[pl.ds(base, 2), rows_of(c)], dst_ref=dst.at[pl.ds(base, 2), rows_of(c)],
+            send_sem=so.at[0], recv_sem=rm.at[2 * c + base // 2],
             device_id={"tp": mate}, device_id_type=MESH)
 
-    def to_peer(src, dst, a, c):
+    def to_peer(src, dst, base, c):
         return pltpu.make_async_remote_copy(
-            src_ref=src.at[a, rows_of(c)], dst_ref=dst.at[a, rows_of(c)],
-            send_sem=sp.at[0], recv_sem=rp.at[QUARTERS * c + a],
+            src_ref=src.at[pl.ds(base, 2), rows_of(c)], dst_ref=dst.at[pl.ds(base, 2), rows_of(c)],
+            send_sem=sp.at[0], recv_sem=rp.at[2 * c + base // 2],
             device_id={"tp": peer}, device_id_type=MESH)
 
     def hop(src, dst, send, recv, t, to):
@@ -131,10 +135,11 @@
             def _():
                 pl.semaphore_wait(barrier, 4)
 
-        @pl.when(is_outer)
-        def _():
-            for c in range(FIRST):
-                to_mate(part, from_mate, a, c).start()
+        if s % 2 == 1:
+            @pl.when(is_outer)
+            def _():
+                for c in range(FIRST if s == 1 else FIRST - LEAD):
+                    to_mate(part, from_mate, base, c).start()
 
     for a in range(QUARTERS):
         r_copy(a).start()
@@ -150,12 +155,18 @@
     def _():
         @pl.loop(FIRST, chunks)
         def _(c):
-            for base in (other, own):
-                for q in range(2):
-                    to_mate(part, from_mate, base + q, c).start()
-
+            to_mate(part, from_mate, other, c).start()
+            to_mate(part, from_mate, own, c - LEAD).start()
+
+        for c in range(chunks - LEAD, chunks):
+            to_mate(part, from_mate, own, c).start()
+
+    gain_copy.wait()
+    lanes = gain_v.shape[1]
+    for g in range(width // lanes):
+        a, at_lane = g * lanes // span, g * lanes % span
+        gain_f[a, :, at_lane:at_lane + lanes] = gain_v[g:g + 1, :].astype(F32)
     for a in range(QUARTERS):
-        gain_f[a] = gain[:, a * span:(a + 1) * span].astype(F32)
         r_copy(a).wait()
         gi_copy(a).wait()
     gacc[...] = jnp.zeros_like(gacc)
@@ -210,54 +221,44 @@
             hop(ys, yr, s3, r3, t, second[v]).start()
             keep[t, :block] = keep[t, :block] + xr[t, :block].astype(F32)
 
-    def wg_copy(t):
-        return pltpu.make_async_copy(
-            wgo.at[t], wg_out.at[:, pl.ds(pl.multiple_of(t * cols, cols), cols)], wg_sem.at[t])
-
     def stage4(j):
         for v in range(2):
             t = 2 * j + v
             hop(ys, yr, s3, r3, t, second[v]).wait_recv()
             wgo[t] = keep[t, :block] + yr[t].astype(F32)
-            wg_copy(t).start()
 
     def pass_on(c):
+        r = rows_of(c)
+        to_mate(part, from_mate, other, c).wait_recv()
         for q in range(2):
             a = other + q
-            to_mate(part, from_mate, a, c).wait_recv()
-            r = rows_of(c)
             part[a, r, :] = (
                 part[a, r, :].astype(F32) + from_mate[a, r, :].astype(F32)).astype(BF16)
-            to_peer(part, from_peer, a, c).start()
+        to_peer(part, from_peer, other, c).start()
 
     def root(c):
+        r = rows_of(c)
+        to_mate(part, from_mate, own, c).wait_recv()
+        to_peer(part, from_peer, own, c).wait_recv()
+        terms = []
         for q in range(2):
             a = own + q
-            to_mate(part, from_mate, a, c).wait_recv()
-            to_peer(part, from_peer, a, c).wait_recv()
-            r = rows_of(c)
             dnormed = part[a, r, :].astype(F32) + from_mate[a, r, :].astype(F32)
             dnormed = dnormed + from_peer[a, r, :].astype(F32)
             ds[a, r, :] = dnormed.astype(BF16)
-            to_mate(ds, ds, a, c).start()
-            to_peer(ds, ds, a, c).start()
-            term = dnormed * (rv[a, r, :].astype(F32) * inv[r, :])
-            gacc[q] += term[:8] + term[8:]
+            terms.append(dnormed * (rv[a, r, :].astype(F32) * inv[r, :]))
+        to_mate(ds, ds, own, c).start()
+        to_peer(ds, ds, own, c).start()
+        for q in range(2):
+            gacc[q] += terms[q][:8] + terms[q][8:]
 
     def forward(c):
-        for q in range(2):
-            a = other + q
-            to_peer(ds, ds, a, c).wait_recv()
-            to_mate(ds, ds, a, c).start()
+        to_peer(ds, ds, other, c).wait_recv()
+        to_mate(ds, ds, other, c).start()
 
     def collect(c):
-        for a in range(QUARTERS):
-            to_mate(part, ds, a, c).wait_recv()
-
-    def out_copy(a, c):
-        return pltpu.make_async_copy(
-            gov.at[a, rows_of(c)], go_out.at[rows_of(c), a * span:(a + 1) * span],
-            out_sem.at[QUARTERS * c + a])
+        for base in (0, 2):
+            to_mate(part, ds, base, c).wait_recv()
 
     def finish(c):
         r = rows_of(c)
@@ -271,7 +272,6 @@
             unit = rv[a, r, :].astype(F32) * scale
             gov[a, r, :] = (
                 giv[a, r, :].astype(F32) + scale * (dunit - unit * mean)).astype(BF16)
-            out_copy(a, c).start()
 
     def g_copy(o):
         return pltpu.make_async_remote_copy(
@@ -299,24 +299,24 @@
         def _():
             pass_on(i)
 
-        @pl.when(jnp.logical_and(is_inner, at(i, 1, chunks + 1)))
-        def _():
-            root(i - 1)
-
-        @pl.when(jnp.logical_and(is_inner, i == chunks))
+        @pl.when(jnp.logical_and(is_inner, at(i, 4, chunks + 4)))
+        def _():
+            forward(i - 4)
+
+        @pl.when(jnp.logical_and(is_inner, at(i, 2, chunks + 2)))
+        def _():
+            root(i - 2)
+
+        @pl.when(jnp.logical_and(is_inner, i == chunks + 1))
         def _():
             for q in range(2):
                 gslot[0, q:q + 1, :] = jnp.sum(gacc[q], axis=0, keepdims=True)
             for o in range(1, n_dp):
                 g_copy(o).start()
 
-        @pl.when(jnp.logical_and(is_inner, at(i, 2, chunks + 2)))
-        def _():
-            forward(i - 2)
-
-        @pl.when(jnp.logical_and(is_inner, at(i, 3, chunks + 3)))
-        def _():
-            finish(i - 3)
+        @pl.when(jnp.logical_and(is_inner, at(i, 5, chunks + 5)))
+        def _():
+            finish(i - 5)
 
         @pl.when(jnp.logical_and(is_outer, i >= LAG))
         def _():
@@ -378,21 +378,30 @@
         z_wait(1)
 
     for a in range(QUARTERS):
-        gg_out[:, a * span:(a + 1) * span] = gz[a // 2, a % 2:a % 2 + 1, :]
+        ggv[:, a * span:(a + 1) * span] = gz[a // 2, a % 2:a % 2 + 1, :]
     pltpu.make_async_remote_copy(
         src_ref=part, dst_ref=ds, send_sem=so.at[0], recv_sem=rm.at[0],
         device_id={"tp": mate}, device_id_type=MESH).wait_send()
-
-    @pl.loop(0, chunks)
-    def _(c):
-        for a in range(QUARTERS):
-            out_copy(a, c).wait()
 
     for t in range(TILES):
         hop(fgs, fgr, s1, r1, t, core_mate).wait_send()
         hop(xs, xr, s2, r2, t, first[t % 2]).wait_send()
         hop(ys, yr, s3, r3, t, second[t % 2]).wait_send()
-        wg_copy(t).wait()
+
+
+def write_out(wgo, ggv, gov, wg_out, gg_out, go_out, sem):
+    cols, span = wgo.shape[2], gov.shape[2]
+    copies = [pltpu.make_async_copy(ggv, gg_out, sem.at[TILES + QUARTERS])]
+    for a in range(QUARTERS):
+        copies.append(pltpu.make_async_copy(
+            gov.at[a], go_out.at[:, a * span:(a + 1) * span], sem.at[TILES + a]))
+    for t in range(TILES):
+        copies.append(pltpu.make_async_copy(
+            wgo.at[t], wg_out.at[:, t * cols:(t + 1) * cols], sem.at[t]))
+    for copy in copies:
+        copy.start()
+    for copy in copies:
+        copy.wait()
 
 
 def fused(n_dp, n_tp, resid, gain, grad_q, w_query, grad_in):
@@ -401,23 +410,24 @@
     chunks = tokens // ROWS
     block, cols, span = heads // n_dp, width // TILES, width // QUARTERS
     any_space = pl.BlockSpec(memory_space=pl.ANY)
-    vmem = pl.BlockSpec(memory_space=pltpu.VMEM)
     dma = lambda n: pltpu.SemaphoreType.DMA((n,))
     wide = lambda: pltpu.VMEM((QUARTERS, tokens, span), BF16)
-    weight_grad, gain_grad, grad_rows = pl.pallas_call(
+    vmem = pl.BlockSpec(memory_space=pltpu.VMEM)
+    held = pl.pallas_call(
         functools.partial(kernel, n_dp, n_tp),
         out_shape=(
-            jax.ShapeDtypeStruct((block, width), F32),
-            jax.ShapeDtypeStruct((1, width), F32),
-            jax.ShapeDtypeStruct((tokens, width), BF16),
+            pltpu.VMEM((TILES, block, cols), F32),
+            pltpu.VMEM((1, width), F32),
+            pltpu.VMEM((QUARTERS, tokens, span), BF16),
         ),
-        in_specs=[any_space, vmem, any_space, any_space, any_space],
-        out_specs=(any_space, vmem, any_space),
+        in_specs=[any_space] * 5,
+        out_specs=(vmem,) * 3,
         scratch_shapes=[
             pltpu.VMEM((QUARTERS, heads, span), BF16),
             wide(),
             pltpu.VMEM((tokens, heads), BF16),
-            wide(), wide(), wide(), wide(), wide(), wide(), wide(),
+            wide(), wide(), wide(), wide(), wide(), wide(),
+            pltpu.VMEM((width // 128, 128), BF16),
             pltpu.VMEM((QUARTERS, 1, span), F32),
             pltpu.VMEM((tokens, 1), F32),
             pltpu.VMEM((heads, tokens), BF16),
@@ -429,19 +439,30 @@
             pltpu.VMEM((TILES, 2 * block, cols), BF16),
             pltpu.VMEM((TILES, block, cols), BF16),
             pltpu.VMEM((TILES, block, cols), BF16),
-            pltpu.VMEM((TILES, block, cols), F32),
             pltpu.VMEM((2, 8, span), F32),
             pltpu.VMEM((n_dp, 2, span), F32),
             pltpu.VMEM((2, 2, span), F32),
-            dma(QUARTERS), dma(1), dma(QUARTERS), dma(QUARTERS), dma(1), dma(1),
-            dma(QUARTERS * chunks), dma(QUARTERS * chunks), dma(QUARTERS * chunks),
-            dma(TILES), dma(TILES), dma(TILES), dma(TILES), dma(TILES), dma(TILES), dma(TILES),
+            dma(QUARTERS), dma(3), dma(QUARTERS), dma(QUARTERS), dma(1), dma(1),
+            dma(2 * chunks), dma(2 * chunks),
+            dma(TILES), dma(TILES), dma(TILES), dma(TILES), dma(TILES), dma(TILES),
             dma(n_dp), dma(n_dp), dma(3), dma(2),
         ],
         compiler_params=pltpu.CompilerParams(
-            collective_id=0, has_side_effects=True, vmem_limit_bytes=60 * 1024 * 1024
+            collective_id=0, has_side_effects=True, vmem_limit_bytes=VMEM_MIB * 1024 * 1024
         ),
-    )(resid, gain.reshape(1, width), grad_q, w_query, grad_in)
+    )(resid, gain.reshape(width // 128, 128), grad_q, w_query, grad_in)
+    weight_grad, gain_grad, grad_rows = pl.pallas_call(
+        write_out,
+        out_shape=(
+            jax.ShapeDtypeStruct((block, width), F32),
+            jax.ShapeDtypeStruct((1, width), F32),
+            jax.ShapeDtypeStruct((tokens, width), BF16),
+        ),
+        in_specs=[vmem] * 3,
+        out_specs=(any_space,) * 3,
+        scratch_shapes=[dma(TILES + QUARTERS + 1)],
+        compiler_params=pltpu.CompilerParams(vmem_limit_bytes=1024 * 1024),
+    )(*held)
     return weight_grad, gain_grad.reshape(width), grad_rows
 
 

time: 74.2 us -> 65.6 us (0.88)
  local copies, waits for them, and re-layouts: 6.05 us -> 0 us
  Pallas kernels: 67.2 us -> 64.8 us
    unnamed x7 -> x0, local copies, waits for them, and re-layouts: 4.74 us -> none
    pallas_call x1 -> x2, Pallas kernels: 67.2 us -> 64.8 us  [the longest x1 62.8 us: fused(): pl.pallas_call(functools.partial(kernel, n_dp, n_tp), out_shape=(pltpu.VM...]
    reshape x1 -> x0, local copies, waits for them, and re-layouts: 1.31 us -> none  [fused(): gain.reshape(1, width)]
where the time goes in v2:
time: 65.6 us; the launch traced here: 65.4 us
  Pallas kernels  64.8 us (99%)
    pallas_call x1, Pallas kernels, fused(): pl.pallas_call(functools.partial(kernel, n_dp, n_tp), out_shape=(pltpu.VM...  62.8 us
    pallas_call x1, Pallas kernels, fused(): pl.pallas_call(write_out, out_shape=(jax.ShapeDtypeStruct((block, width),...  1.94 us

profile of v2, /device:TPU:0, one launch (start us, length us, event | category | flops | bytes accessed | tf_op | source)
XLA Modules:
  0.0 65.4 jit_solution(5455959036053539637)
XLA Ops:
  0.6 62.8 %shard_map.76 = (f32[8,96,512]{2,1,0:T(8,128)S(1)}, f32[1,4096]{1,0:T(1,128)S(1)}, bf16[4,256,1024]{2,1,0:T(8,128)(2,1)S(1)}) custom-call(bf16[256,4096]{1,0:T(8,128)(2,1)} %resid.1, bf16[32,128]{1,0:T(8,128)(2,1)} %bitcast.2, bf16[256,768]{1,0:T(8,128)(2,1)} %grad_q.1, bf16[768,4096]{1,0:T(8,128)(2,1)} %w_query.1, bf16[256,4096]{1,0:T(8,128)(2,1)} %grad_in.1), custom_call_target="tpu_custom_call" | custom-call | tf_op jit(solution)/shard_map/pallas_call | solution.py:416
  63.5 1.9 %shard_map.77 = (f32[96,4096]{1,0:T(8,128)}, f32[1,4096]{1,0:T(1,128)}, bf16[256,4096]{1,0:T(8,128)(2,1)}) custom-call(f32[8,96,512]{2,1,0:T(8,128)S(1)} %get-tuple-element.9.wgo, f32[1,4096]{1,0:T(1,128)S(1)} %get-tuple-element.10.ggv, bf16[4,256,1024]{2,1,0:T(8,128)(2,1)S(1)} %get-tuple-element.11.gov), custom_call_target="tpu_custom_call" | custom-call | tf_op jit(solution)/shard_map/pallas_call | solution.py:454

commit v3 on v2

--- a/solution.py
+++ b/solution.py
@@ -17,6 +17,7 @@
 FIRST = LEAD + 1
 VMEM_MIB = 52
 LAG = 6
+MIDDLE = 8
 
 
 def norm_rows(rows_bf, gain_f):
@@ -44,10 +45,22 @@
     return (weight_grad, gain_grad, grad_rows)
 
 
-def kernel(n_dp, n_tp, resid, gain, grad_q, w_query, grad_in, wgo, ggv, gov,
-           wv, rv, gqv, giv, nv, part, from_mate, from_peer, ds, gain_v, gain_f, inv, gq_t, gq_p,
+def residual_rows(summed, rows, above, scale, gain_f, out, at):
+    span = gain_f.shape[2]
+    total = jnp.zeros((ROWS, span), F32)
+    for a in range(QUARTERS):
+        total = total + summed(a).astype(F32) * gain_f[a] * (rows(a).astype(F32) * scale)
+    mean = jnp.sum(total, axis=-1, keepdims=True) * (1.0 / (QUARTERS * span))
+    for a in range(QUARTERS):
+        dunit = summed(a).astype(F32) * gain_f[a]
+        unit = rows(a).astype(F32) * scale
+        out[a, at, :] = (above(a).astype(F32) + scale * (dunit - unit * mean)).astype(BF16)
+
+
+def kernel(n_dp, n_tp, resid, gain, grad_q, w_query, grad_in, wgo, ggv, gov, ds_end, rv_end, gi_end, inv_end, gain_f,
+           wv, rv, gqv, giv, nv, part, from_mate, from_peer, ds, gain_v, inv, gq_t, gq_p,
            fgs, fgr, keep, xs, xr, ys, yr, gacc, gslot, gz,
-           w_sem, in_sem, r_sem, gi_sem, so, sp, rm, rp,
+           gqx, w_sem, in_sem, r_sem, gi_sem, so, sp, rm, rp, sq, rq, sx, rx,
            s1, r1, s2, r2, s3, r3, sg, rg, sz, rz):
     dp, tp = lax.axis_index("dp"), lax.axis_index("tp")
     _, tokens, span = rv.shape
@@ -65,14 +78,24 @@
     core_mate = dp + 1 - 2 * core
     x_mate = dp + 2 - 4 * xx
     y_mate = dp + 4 - 8 * yy
-    own, other = 2 * h, 2 - 2 * h
+    own, other = h, 1 - h
+    last = chunks - 1
+    count = last + 2 * core
+
+    def nth(k):
+        moved = jnp.where(k < MIDDLE, k, jnp.where(k == MIDDLE, chunks, k - 1))
+        return jnp.where(core == 1, moved, k)
+
     turns = ((other, 0), (other, 1), (own, 0), (own, 1))
 
     def span_of(a):
         return pl.ds(pl.multiple_of(a * span, span), span)
 
+    def lanes_of(q):
+        return slice(q * span, (q + 1) * span)
+
     def w_copy(s):
-        a = turns[s][0] + turns[s][1]
+        a = 2 * turns[s][0] + turns[s][1]
         return pltpu.make_async_copy(w_query.at[:, span_of(a)], wv.at[a], w_sem.at[s])
 
     def r_copy(a):
@@ -102,16 +125,16 @@
     def rows_of(c):
         return pl.ds(pl.multiple_of(c * ROWS, ROWS), ROWS)
 
-    def to_mate(src, dst, base, c):
+    def to_mate(src, dst, half, c):
         return pltpu.make_async_remote_copy(
-            src_ref=src.at[pl.ds(base, 2), rows_of(c)], dst_ref=dst.at[pl.ds(base, 2), rows_of(c)],
-            send_sem=so.at[0], recv_sem=rm.at[2 * c + base // 2],
+            src_ref=src.at[half, rows_of(c)], dst_ref=dst.at[half, rows_of(c)],
+            send_sem=so.at[0], recv_sem=rm.at[2 * c + half],
             device_id={"tp": mate}, device_id_type=MESH)
 
-    def to_peer(src, dst, base, c):
+    def to_peer(src, dst, half, c):
         return pltpu.make_async_remote_copy(
-            src_ref=src.at[pl.ds(base, 2), rows_of(c)], dst_ref=dst.at[pl.ds(base, 2), rows_of(c)],
-            send_sem=sp.at[0], recv_sem=rp.at[2 * c + base // 2],
+            src_ref=src.at[half, rows_of(c)], dst_ref=dst.at[half, rows_of(c)],
+            send_sem=sp.at[0], recv_sem=rp.at[2 * c + half],
             device_id={"tp": peer}, device_id_type=MESH)
 
     def hop(src, dst, send, recv, t, to):
@@ -122,11 +145,10 @@
     gq_copy.wait()
     head = FIRST * ROWS
     for s, (base, q) in enumerate(turns):
-        a = base + q
         w_copy(s).wait()
-        part[a, :head, :] = jnp.dot(
-            gqv[:head, :], wv[a], preferred_element_type=F32).astype(BF16)
-        if s == 0:
+        part[base, :head, lanes_of(q)] = jnp.dot(
+            gqv[:head, :], wv[2 * base + q], preferred_element_type=F32).astype(BF16)
+        if s == 1:
             @pl.when(is_inner)
             def _():
                 pl.semaphore_wait(barrier, 5)
@@ -141,25 +163,35 @@
                 for c in range(FIRST if s == 1 else FIRST - LEAD):
                     to_mate(part, from_mate, base, c).start()
 
+    ends = pltpu.make_async_remote_copy(
+        src_ref=gqv.at[tokens - ROWS:], dst_ref=gqx, send_sem=sq.at[0], recv_sem=rq.at[0],
+        device_id={"dp": core_mate}, device_id_type=MESH)
+    pl.when(core == 0)(ends.start)
     for a in range(QUARTERS):
         r_copy(a).start()
     for a in range(QUARTERS):
         gi_copy(a).start()
 
     for base, q in turns:
-        a = base + q
-        part[a, head:, :] = jnp.dot(
-            gqv[head:, :], wv[a], preferred_element_type=F32).astype(BF16)
+        part[base, head:tokens, lanes_of(q)] = jnp.dot(
+            gqv[head:, :], wv[2 * base + q], preferred_element_type=F32).astype(BF16)
+
+    @pl.when(core == 1)
+    def _():
+        ends.wait_recv()
+        for base, q in turns:
+            part[base, tokens:, lanes_of(q)] = jnp.dot(
+                gqx[...], wv[2 * base + q], preferred_element_type=F32).astype(BF16)
 
     @pl.when(is_outer)
     def _():
-        @pl.loop(FIRST, chunks)
-        def _(c):
-            to_mate(part, from_mate, other, c).start()
-            to_mate(part, from_mate, own, c - LEAD).start()
-
-        for c in range(chunks - LEAD, chunks):
-            to_mate(part, from_mate, own, c).start()
+        @pl.loop(FIRST, count)
+        def _(k):
+            to_mate(part, from_mate, other, nth(k)).start()
+            to_mate(part, from_mate, own, nth(k - LEAD)).start()
+
+        for j in range(LEAD):
+            to_mate(part, from_mate, own, nth(count - LEAD + j)).start()
 
     gain_copy.wait()
     lanes = gain_v.shape[1]
@@ -231,22 +263,24 @@
         r = rows_of(c)
         to_mate(part, from_mate, other, c).wait_recv()
         for q in range(2):
-            a = other + q
-            part[a, r, :] = (
-                part[a, r, :].astype(F32) + from_mate[a, r, :].astype(F32)).astype(BF16)
+            at = (other, r, lanes_of(q))
+            part[at] = (part[at].astype(F32) + from_mate[at].astype(F32)).astype(BF16)
         to_peer(part, from_peer, other, c).start()
 
     def root(c):
         r = rows_of(c)
         to_mate(part, from_mate, own, c).wait_recv()
         to_peer(part, from_peer, own, c).wait_recv()
+        mine = jnp.minimum(c, last)
+        keep_it = jnp.where(c == chunks, 0.0, 1.0)
         terms = []
         for q in range(2):
-            a = own + q
-            dnormed = part[a, r, :].astype(F32) + from_mate[a, r, :].astype(F32)
-            dnormed = dnormed + from_peer[a, r, :].astype(F32)
-            ds[a, r, :] = dnormed.astype(BF16)
-            terms.append(dnormed * (rv[a, r, :].astype(F32) * inv[r, :]))
+            at = (own, r, lanes_of(q))
+            dnormed = part[at].astype(F32) + from_mate[at].astype(F32)
+            dnormed = dnormed + from_peer[at].astype(F32)
+            ds[at] = dnormed.astype(BF16)
+            unit = rv[2 * own + q, rows_of(mine), :].astype(F32) * inv[rows_of(mine), :]
+            terms.append(dnormed * unit * keep_it)
         to_mate(ds, ds, own, c).start()
         to_peer(ds, ds, own, c).start()
         for q in range(2):
@@ -256,22 +290,33 @@
         to_peer(ds, ds, other, c).wait_recv()
         to_mate(ds, ds, other, c).start()
 
+    def give(half):
+        return pltpu.make_async_remote_copy(
+            src_ref=ds.at[half, rows_of(chunks)], dst_ref=ds.at[half, rows_of(last)],
+            send_sem=sx.at[half], recv_sem=rx.at[half],
+            device_id={"dp": core_mate}, device_id_type=MESH)
+
+    def give_both():
+        for half in range(2):
+            give(half).start()
+
+    def absorb():
+        give(own).wait_recv()
+        r = rows_of(last)
+        for q in range(2):
+            unit = rv[2 * own + q, r, :].astype(F32) * inv[r, :]
+            term = ds[own, r, lanes_of(q)].astype(F32) * unit
+            gacc[q] += term[:8] + term[8:]
+
     def collect(c):
-        for base in (0, 2):
-            to_mate(part, ds, base, c).wait_recv()
+        for half in range(2):
+            to_mate(part, ds, half, c).wait_recv()
 
     def finish(c):
         r = rows_of(c)
-        scale = inv[r, :]
-        total = jnp.zeros((ROWS, span), F32)
-        for a in range(QUARTERS):
-            total = total + ds[a, r, :].astype(F32) * gain_f[a] * (rv[a, r, :].astype(F32) * scale)
-        mean = jnp.sum(total, axis=-1, keepdims=True) * (1.0 / width)
-        for a in range(QUARTERS):
-            dunit = ds[a, r, :].astype(F32) * gain_f[a]
-            unit = rv[a, r, :].astype(F32) * scale
-            gov[a, r, :] = (
-                giv[a, r, :].astype(F32) + scale * (dunit - unit * mean)).astype(BF16)
+        residual_rows(
+            lambda a: ds[a // 2, r, lanes_of(a % 2)], lambda a: rv[a, r, :],
+            lambda a: giv[a, r, :], inv[r, :], gain_f, gov, r)
 
     def g_copy(o):
         return pltpu.make_async_remote_copy(
@@ -290,38 +335,57 @@
             src_ref=gz.at[which], dst_ref=gz.at[which], send_sem=sz.at[0], recv_sem=rz.at[which],
             device_id={"tp": mate}, device_id_type=MESH).wait_recv()
 
+    def sent(sem):
+        for which, rows in ((0, tokens - ROWS), (1, tokens + ROWS)):
+            @pl.when(core == which)
+            def _():
+                pltpu.make_async_remote_copy(
+                    src_ref=part.at[:, :rows], dst_ref=ds.at[:, :rows], send_sem=sem.at[0],
+                    recv_sem=rm.at[0], device_id={"tp": mate}, device_id_type=MESH).wait_send()
+
     def at(i, lo, hi):
         return jnp.logical_and(i >= lo, i < hi)
 
+    extra = jnp.logical_and(core == 1, is_inner)
+
     @pl.loop(0, chunks + LAG)
     def _(i):
-        @pl.when(jnp.logical_and(is_inner, i < chunks))
-        def _():
-            pass_on(i)
-
-        @pl.when(jnp.logical_and(is_inner, at(i, 4, chunks + 4)))
-        def _():
-            forward(i - 4)
-
-        @pl.when(jnp.logical_and(is_inner, at(i, 2, chunks + 2)))
-        def _():
-            root(i - 2)
-
-        @pl.when(jnp.logical_and(is_inner, i == chunks + 1))
+        @pl.when(jnp.logical_and(is_inner, i < count))
+        def _():
+            pass_on(nth(i))
+
+        @pl.when(jnp.logical_and(is_inner, at(i, 4, count + 4)))
+        def _():
+            forward(nth(i - 4))
+
+        @pl.when(jnp.logical_and(extra, i == MIDDLE + 4))
+        def _():
+            give_both()
+
+        @pl.when(jnp.logical_and(jnp.logical_and(is_inner, core == 0), i == chunks - 1))
+        def _():
+            absorb()
+
+        @pl.when(jnp.logical_and(is_inner, at(i, 2, count + 2)))
+        def _():
+            root(nth(i - 2))
+
+        @pl.when(jnp.logical_and(is_inner, i == count + 1))
         def _():
             for q in range(2):
                 gslot[0, q:q + 1, :] = jnp.sum(gacc[q], axis=0, keepdims=True)
             for o in range(1, n_dp):
                 g_copy(o).start()
 
-        @pl.when(jnp.logical_and(is_inner, at(i, 5, chunks + 5)))
-        def _():
-            finish(i - 5)
-
-        @pl.when(jnp.logical_and(is_outer, i >= LAG))
-        def _():
-            collect(i - LAG)
-            finish(i - LAG)
+        @pl.when(jnp.logical_and(is_inner, at(i, 5, count + 5)))
+        def _():
+            pl.when(nth(i - 5) < last)(lambda: finish(nth(i - 5)))
+
+        @pl.when(jnp.logical_and(is_outer, at(i, LAG, last + core + LAG)))
+        def _():
+            collect(nth(i - LAG))
+            pl.when(nth(i - LAG) < last)(lambda: finish(nth(i - LAG)))
+            pl.when(nth(i - LAG) == chunks)(give_both)
 
         @pl.when(i == 0)
         def _():
@@ -330,6 +394,12 @@
         @pl.when(i == 1)
         def _():
             pl.loop(9, 13)(norm)
+
+        @pl.when(i == 3)
+        def _():
+            rv_end[...] = rv[:, tokens - ROWS:, :]
+            gi_end[...] = giv[:, tokens - ROWS:, :]
+            inv_end[...] = inv[tokens - ROWS:, :]
 
         @pl.when(i == 2)
         def _():
@@ -368,9 +438,22 @@
             z_copy(i).wait_send()
         for o in range(1, n_dp):
             g_copy(o).wait_send()
-        pltpu.make_async_remote_copy(
-            src_ref=part, dst_ref=ds, send_sem=sp.at[0], recv_sem=rp.at[0],
-            device_id={"tp": peer}, device_id_type=MESH).wait_send()
+        sent(sp)
+
+    pl.when(jnp.logical_and(is_outer, core == 1))(lambda: collect(last))
+
+    @pl.when(core == 0)
+    def _():
+        ends.wait_send()
+        pl.when(is_outer)(lambda: give(own).wait_recv())
+        give(other).wait_recv()
+
+    @pl.when(core == 1)
+    def _():
+        for half in range(2):
+            give(half).wait_send()
+
+    ds_end[...] = ds[:, tokens - ROWS:tokens, :]
 
     @pl.when(is_outer)
     def _():
@@ -379,9 +462,7 @@
 
     for a in range(QUARTERS):
         ggv[:, a * span:(a + 1) * span] = gz[a // 2, a % 2:a % 2 + 1, :]
-    pltpu.make_async_remote_copy(
-        src_ref=part, dst_ref=ds, send_sem=so.at[0], recv_sem=rm.at[0],
-        device_id={"tp": mate}, device_id_type=MESH).wait_send()
+    sent(so)
 
     for t in range(TILES):
         hop(fgs, fgr, s1, r1, t, core_mate).wait_send()
@@ -389,17 +470,31 @@
         hop(ys, yr, s3, r3, t, second[t % 2]).wait_send()
 
 
-def write_out(wgo, ggv, gov, wg_out, gg_out, go_out, sem):
+def write_out(wgo, ggv, gov, ds_end, rv_end, gi_end, inv_end, gain_f,
+              wg_out, gg_out, go_out, end, sem):
     cols, span = wgo.shape[2], gov.shape[2]
-    copies = [pltpu.make_async_copy(ggv, gg_out, sem.at[TILES + QUARTERS])]
-    for a in range(QUARTERS):
-        copies.append(pltpu.make_async_copy(
-            gov.at[a], go_out.at[:, a * span:(a + 1) * span], sem.at[TILES + a]))
-    for t in range(TILES):
-        copies.append(pltpu.make_async_copy(
-            wgo.at[t], wg_out.at[:, t * cols:(t + 1) * cols], sem.at[t]))
+    done = gov.shape[1] - ROWS
+    copies = [
+        pltpu.make_async_copy(
+            gov.at[a, :done], go_out.at[:done, a * span:(a + 1) * span], sem.at[a])
+        for a in range(QUARTERS)
+    ]
+    copies += [
+        pltpu.make_async_copy(
+            wgo.at[t], wg_out.at[:, t * cols:(t + 1) * cols], sem.at[QUARTERS + t])
+        for t in range(TILES)
+    ]
+    copies.append(pltpu.make_async_copy(ggv, gg_out, sem.at[QUARTERS + TILES]))
     for copy in copies:
         copy.start()
+    residual_rows(
+        lambda a: ds_end[a // 2, :, a % 2 * span:(a % 2 + 1) * span], lambda a: rv_end[a],
+        lambda a: gi_end[a], inv_end[...], gain_f, end, slice(0, ROWS))
+    for a in range(QUARTERS):
+        copies.append(pltpu.make_async_copy(
+            end.at[a], go_out.at[done:, a * span:(a + 1) * span],
+            sem.at[QUARTERS + TILES + 1 + a]))
+        copies[-1].start()
     for copy in copies:
         copy.wait()
 
@@ -412,6 +507,7 @@
     any_space = pl.BlockSpec(memory_space=pl.ANY)
     dma = lambda n: pltpu.SemaphoreType.DMA((n,))
     wide = lambda: pltpu.VMEM((QUARTERS, tokens, span), BF16)
+    halves = lambda: pltpu.VMEM((2, tokens + ROWS, 2 * span), BF16)
     vmem = pl.BlockSpec(memory_space=pltpu.VMEM)
     held = pl.pallas_call(
         functools.partial(kernel, n_dp, n_tp),
@@ -419,16 +515,20 @@
             pltpu.VMEM((TILES, block, cols), F32),
             pltpu.VMEM((1, width), F32),
             pltpu.VMEM((QUARTERS, tokens, span), BF16),
+            pltpu.VMEM((2, ROWS, 2 * span), BF16),
+            pltpu.VMEM((QUARTERS, ROWS, span), BF16),
+            pltpu.VMEM((QUARTERS, ROWS, span), BF16),
+            pltpu.VMEM((ROWS, 1), F32),
+            pltpu.VMEM((QUARTERS, 1, span), F32),
         ),
         in_specs=[any_space] * 5,
-        out_specs=(vmem,) * 3,
+        out_specs=(vmem,) * 8,
         scratch_shapes=[
             pltpu.VMEM((QUARTERS, heads, span), BF16),
             wide(),
             pltpu.VMEM((tokens, heads), BF16),
-            wide(), wide(), wide(), wide(), wide(), wide(),
+            wide(), wide(), halves(), halves(), halves(), halves(),
             pltpu.VMEM((width // 128, 128), BF16),
-            pltpu.VMEM((QUARTERS, 1, span), F32),
             pltpu.VMEM((tokens, 1), F32),
             pltpu.VMEM((heads, tokens), BF16),
             pltpu.VMEM((2, 2, 4 * block, tokens), BF16),
@@ -442,8 +542,9 @@
             pltpu.VMEM((2, 8, span), F32),
             pltpu.VMEM((n_dp, 2, span), F32),
             pltpu.VMEM((2, 2, span), F32),
+            pltpu.VMEM((ROWS, heads), BF16),
             dma(QUARTERS), dma(3), dma(QUARTERS), dma(QUARTERS), dma(1), dma(1),
-            dma(2 * chunks), dma(2 * chunks),
+            dma(2 * chunks + 2), dma(2 * chunks + 2), dma(1), dma(1), dma(2), dma(2),
             dma(TILES), dma(TILES), dma(TILES), dma(TILES), dma(TILES), dma(TILES),
             dma(n_dp), dma(n_dp), dma(3), dma(2),
         ],
@@ -458,10 +559,11 @@
             jax.ShapeDtypeStruct((1, width), F32),
             jax.ShapeDtypeStruct((tokens, width), BF16),
         ),
-        in_specs=[vmem] * 3,
+        in_specs=[vmem] * 8,
         out_specs=(any_space,) * 3,
-        scratch_shapes=[dma(TILES + QUARTERS + 1)],
-        compiler_params=pltpu.CompilerParams(vmem_limit_bytes=1024 * 1024),
+        scratch_shapes=[
+            pltpu.VMEM((QUARTERS, ROWS, span), BF16), dma(TILES + 2 * QUARTERS + 1)],
+        compiler_params=pltpu.CompilerParams(vmem_limit_bytes=2 * 1024 * 1024),
     )(*held)
     return weight_grad, gain_grad.reshape(width), grad_rows
 

time: 65.6 us -> 64.9 us (0.989)
  Pallas kernels: 64.8 us -> 64.1 us
    pallas_call x1, Pallas kernels: 62.8 us -> 62.1 us  [fused(): pl.pallas_call(functools.partial(kernel, n_dp, n_tp), out_shape=(pltpu.VM...]
where the time goes in v3:
time: 64.9 us; the launch traced here: 64.8 us
  Pallas kernels  64.1 us (99%)
    pallas_call x1, Pallas kernels, fused(): pl.pallas_call(functools.partial(kernel, n_dp, n_tp), out_shape=(pltpu.VM...  62.1 us
    pallas_call x1, Pallas kernels, fused(): pl.pallas_call(write_out, out_shape=(jax.ShapeDtypeStruct((block, width),...  1.99 us

profile of v3, /device:TPU:0, one launch (start us, length us, event | category | flops | bytes accessed | tf_op | source)
XLA Modules:
  0.0 64.8 jit_solution(455356239507807223)
XLA Ops:
  0.6 62.1 %shard_map.76 = (f32[8,96,512]{2,1,0:T(8,128)S(1)}, f32[1,4096]{1,0:T(1,128)S(1)}, bf16[4,256,1024]{2,1,0:T(8,128)(2,1)S(1)}, bf16[2,16,2048]{2,1,0:T(8,128)(2,1...) custom-call(bf16[256,4096]{1,0:T(8,128)(2,1)} %resid.1, ...), custom_call_target="tpu_custom_call" | custom-call | tf_op jit(solution)/shard_map/pallas_call | solution.py:512
  62.8 2.0 %shard_map.77 = (f32[96,4096]{1,0:T(8,128)}, f32[1,4096]{1,0:T(1,128)}, bf16[256,4096]{1,0:T(8,128)(2,1)}) custom-call(f32[8,96,512]{2,1,0:T(8,128)S(1)} %get-tuple-element.14.wgo, f32[1,4096]{1,0:T(1,128)S(1)} %get-tuple-element.15.ggv, bf16[4,256,1024]{2,1,0:T(8,128)(2,1)S(1)} %get-tuple-element.16.gov, bf16[2,16,2048]{2,1,0:T(8,128)(2,1)S(1)} %get-tuple-element.17.ds_end, ...), custom_call_target="tpu_custom_call" | custom-call | tf_op jit(solution)/shard_map/pallas_call | solution.py:555

commit v4 on v3

--- a/solution.py
+++ b/solution.py
@@ -389,11 +389,11 @@
 
         @pl.when(i == 0)
         def _():
-            pl.loop(0, 9)(norm)
+            pl.loop(0, 5)(norm)
 
         @pl.when(i == 1)
         def _():
-            pl.loop(9, 13)(norm)
+            pl.loop(5, 11)(norm)
 
         @pl.when(i == 3)
         def _():
@@ -403,7 +403,7 @@
 
         @pl.when(i == 2)
         def _():
-            pl.loop(13, chunks)(norm)
+            pl.loop(11, chunks)(norm)
             regroup()
 
         @pl.when(at(i, 3, 5))

time: 64.9 us -> 64.5 us (level)
  no operation moved by 1% of the time
where the time goes in v4:
time: 64.5 us; the launch traced here: 64.4 us
  Pallas kernels  63.7 us (99%)
    pallas_call x1, Pallas kernels, fused(): pl.pallas_call(functools.partial(kernel, n_dp, n_tp), out_shape=(pltpu.VM...  61.8 us
    pallas_call x1, Pallas kernels, fused(): pl.pallas_call(write_out, out_shape=(jax.ShapeDtypeStruct((block, width),...  1.99 us

profile of v4, /device:TPU:0, one launch (start us, length us, event | category | flops | bytes accessed | tf_op | source)
XLA Modules:
  0.0 64.4 jit_solution(15092846906633719814)
XLA Ops:
  0.6 61.8 %shard_map.76 = (f32[8,96,512]{2,1,0:T(8,128)S(1)}, f32[1,4096]{1,0:T(1,128)S(1)}, bf16[4,256,1024]{2,1,0:T(8,128)(2,1)S(1)}, bf16[2,16,2048]{2,1,0:T(8,128)(2,1...) custom-call(bf16[256,4096]{1,0:T(8,128)(2,1)} %resid.1, ...), custom_call_target="tpu_custom_call" | custom-call | tf_op jit(solution)/shard_map/pallas_call | solution.py:512
  62.4 2.0 %shard_map.77 = (f32[96,4096]{1,0:T(8,128)}, f32[1,4096]{1,0:T(1,128)}, bf16[256,4096]{1,0:T(8,128)(2,1)}) custom-call(f32[8,96,512]{2,1,0:T(8,128)S(1)} %get-tuple-element.14.wgo, f32[1,4096]{1,0:T(1,128)S(1)} %get-tuple-element.15.ggv, bf16[4,256,1024]{2,1,0:T(8,128)(2,1)S(1)} %get-tuple-element.16.gov, bf16[2,16,2048]{2,1,0:T(8,128)(2,1)S(1)} %get-tuple-element.17.ds_end, ...), custom_call_target="tpu_custom_call" | custom-call | tf_op jit(solution)/shard_map/pallas_call | solution.py:555
